TPU v7x, 64 devices: a 2x2x8 block of a 4x4x8 slice. The times are simulated.
64 devices in a mesh: data: 4 (over x, y), time: 16 (over z, core).
Axes of the slice: x: 2, y: 2, z: 8, core: 2. Of those that a mesh axis runs over, the one named last changes fastest.
The devices are a block of a 4x4x8 slice.
Arguments:
- x_init: float32 [4, 4096, 64], P('data'), parts along dimension 0
- w_in: bfloat16 [64, 1536], replicated
- w_out: bfloat16 [1536, 64], replicated
- mod_scale: bfloat16 [32, 1536], P('time')
- mod_shift: bfloat16 [32, 1536], P('time')
- step_size: float32 [32], P('time')
- noise_inc: float32 [32, 4, 4096, 64], P('time', 'data'), parts along dimension 1
Outputs:
- output: float32 [32, 4, 4096, 64], P('time', 'data'), parts along dimension 1
There are 4 independent parts. A program takes and returns all parts, laid end to end along the dimension named above; an argument that names none is the same for every part.
All inputs are finite; a program needn't handle non-finite values.
Results may differ from a plain program's by a relative error of at most 0.001.
Values are sent between devices in bfloat16 or wider.
A program may use at most 768 MiB of HBM per device.

v0:
```python
import jax
import jax.numpy as jnp
from jax import lax
from jax.sharding import PartitionSpec as P

SWEEPS = 8


def local_drift(latents, w_in, w_out, scale_f, shift_f, step_size):
    pre_act = jnp.einsum("tbnc,cd->tbnd", latents.astype(jnp.bfloat16), w_in, preferred_element_type=jnp.float32)
    hidden = pre_act * scale_f[:, None, None, :] + shift_f[:, None, None, :]
    gelu_out = jax.nn.gelu(hidden, approximate=True).astype(jnp.bfloat16)
    proj_out = jnp.einsum("tbnd,dc->tbnc", gelu_out, w_out, preferred_element_type=jnp.float32)
    return proj_out * step_size[:, None, None, None]


def solution(mesh):
    n_time = mesh.shape["time"]
    shifts = [2 ** level for level in range(12) if 2 ** level < n_time]

    def body(x_init, w_in, w_out, mod_scale, mod_shift, step_size, noise_inc):
        scale_f = 1.0 + mod_scale.astype(jnp.float32)
        shift_f = mod_shift.astype(jnp.float32)
        latents = jnp.broadcast_to(x_init[None], noise_inc.shape)
        for sweep_num in range(SWEEPS):
            increments = local_drift(latents, w_in, w_out, scale_f, shift_f, step_size) + noise_inc
            running = jnp.cumsum(increments, axis=0)
            dev_total = running[-1]
            prefix = dev_total
            for distance in shifts:
                moved = lax.ppermute(prefix, "time", [(source, source + distance) for source in range(n_time - distance)])
                prefix = prefix + moved
            latents = x_init[None] + (prefix - dev_total)[None] + (running - increments)
        return latents

    return jax.shard_map(
        body,
        mesh=mesh,
        in_specs=(P("data"), P(), P(), P("time"), P("time"), P("time"), P("time", "data")),
        out_specs=P("time", "data"),
        check_vma=False,
    )
```

profile of v0, /device:TPU:55, one launch (start us, length us, event | category | flops | bytes accessed | tf_op | source)
XLA Modules:
  0.0 1680.4 jit_solution(7794079781055765275)
XLA Ops:
  79.3 67.3 %collective-permute-done.2 = f32[1,4096,64]{1,2,0:T(8,128)S(1)} collective-permute-done((f32[1,4096,64]{1,2,0:T(8,128)S(1)}, f32[1,4096,64]{1,2,0:T(8,128)S(1)}, u32[]{:S(2)}, u32[]{:S(2)}) %collective-permute-start.2) | collective-permute-done | bytes 1048608 | tf_op jit(solution)/shard_map/ppermute | solution.py:31
  152.9 43.9 %collective-permute-done.3 = f32[1,4096,64]{1,2,0:T(8,128)S(1)} collective-permute-done((f32[1,4096,64]{1,2,0:T(8,128)S(1)}, f32[1,4096,64]{1,2,0:T(8,128)S(1)}, u32[]{:S(2)}, u32[]{:S(2)}) %collective-permute-start.3) | collective-permute-done | bytes 1048608 | tf_op jit(solution)/shard_map/ppermute | solution.py:31
  198.3 25.4 %fusion.111 = f32[2,1,4096,64]{2,3,0,1:T(8,128)} fusion(f32[2,1536]{1,0:T(2,128)S(1)} %convert_element_type.67, f32[2,1536]{1,0:T(2,128)S(1)} %convert_add_fusion, f32[2,1,4096,64]{2,3,1,0:T(8,128)} %param.13, f32[2,1,4096,64]{2,3,0,1:T(8,128)S(1)} %fusion.269, f32[2,1,4096,64]{2,3,0,1:T(8,128)} %fusion.102, f32[4096,64]{0,1:T(8,128)S(1)} %add_bitcast_fusion.8, ...), kind=kOutput, calls=%fused_computation.93 | convolution fusion | flops 3362258944 | bytes 9854984 | tf_op jit(solution)/shard_map/tbnd,dc->tbnc/dot_general | solution.py:13
  264.5 55.1 %collective-permute-done.6 = f32[1,4096,64]{1,2,0:T(8,128)S(1)} collective-permute-done((f32[1,4096,64]{1,2,0:T(8,128)S(1)}, f32[1,4096,64]{1,2,0:T(8,128)S(1)}, u32[]{:S(2)}, u32[]{:S(2)}) %collective-permute-start.6) | collective-permute-done | bytes 1048608 | tf_op jit(solution)/shard_map/ppermute | solution.py:31
  319.7 48.0 %collective-permute-start.7 = (f32[1,4096,64]{1,2,0:T(8,128)S(1)}, f32[1,4096,64]{1,2,0:T(8,128)S(1)}, u32[]{:S(2)}, u32[]{:S(2)}) collective-permute-start(f32[1,4096,64]{1,2,0:T(8,128)S(1)} %add.421), channel_id=1, source_target_pairs={{0,8},{1,9},{2,10},{3,11},{4,12},{5,13},{6,14},{7,15},{16,24},{17,... | collective-permute-start | bytes 3145736 | tf_op jit(solution)/shard_map/ppermute | solution.py:31
  367.8 40.5 %collective-permute-done.7 = f32[1,4096,64]{1,2,0:T(8,128)S(1)} collective-permute-done((f32[1,4096,64]{1,2,0:T(8,128)S(1)}, f32[1,4096,64]{1,2,0:T(8,128)S(1)}, u32[]{:S(2)}, u32[]{:S(2)}) %collective-permute-start.7) | collective-permute-done | bytes 1048608 | tf_op jit(solution)/shard_map/ppermute | solution.py:31
  476.1 54.9 %collective-permute-done.10 = f32[1,4096,64]{1,2,0:T(8,128)S(1)} collective-permute-done((f32[1,4096,64]{1,2,0:T(8,128)S(1)}, f32[1,4096,64]{1,2,0:T(8,128)S(1)}, u32[]{:S(2)}, u32[]{:S(2)}) %collective-permute-start.10) | collective-permute-done | bytes 1048608 | tf_op jit(solution)/shard_map/ppermute | solution.py:31
  531.1 47.6 %collective-permute-start.11 = (f32[1,4096,64]{1,2,0:T(8,128)S(1)}, f32[1,4096,64]{1,2,0:T(8,128)S(1)}, u32[]{:S(2)}, u32[]{:S(2)}) collective-permute-start(f32[1,4096,64]{1,2,0:T(8,128)S(1)} %add.433), channel_id=1, source_target_pairs={{0,8},{1,9},{2,10},{3,11},{4,12},{5,13},{6,14},{7,15},{16,24},{17,... | collective-permute-start | bytes 3145736 | tf_op jit(solution)/shard_map/ppermute | solution.py:31
  578.8 40.9 %collective-permute-done.11 = f32[1,4096,64]{1,2,0:T(8,128)S(1)} collective-permute-done((f32[1,4096,64]{1,2,0:T(8,128)S(1)}, f32[1,4096,64]{1,2,0:T(8,128)S(1)}, u32[]{:S(2)}, u32[]{:S(2)}) %collective-permute-start.11) | collective-permute-done | bytes 1048608 | tf_op jit(solution)/shard_map/ppermute | solution.py:31
  687.3 55.1 %collective-permute-done.14 = f32[1,4096,64]{1,2,0:T(8,128)S(1)} collective-permute-done((f32[1,4096,64]{1,2,0:T(8,128)S(1)}, f32[1,4096,64]{1,2,0:T(8,128)S(1)}, u32[]{:S(2)}, u32[]{:S(2)}) %collective-permute-start.14) | collective-permute-done | bytes 1048608 | tf_op jit(solution)/shard_map/ppermute | solution.py:31
  742.6 47.6 %collective-permute-start.15 = (f32[1,4096,64]{1,2,0:T(8,128)S(1)}, f32[1,4096,64]{1,2,0:T(8,128)S(1)}, u32[]{:S(2)}, u32[]{:S(2)}) collective-permute-start(f32[1,4096,64]{1,2,0:T(8,128)S(1)} %add.445), channel_id=1, source_target_pairs={{0,8},{1,9},{2,10},{3,11},{4,12},{5,13},{6,14},{7,15},{16,24},{17,... | collective-permute-start | bytes 3145736 | tf_op jit(solution)/shard_map/ppermute | solution.py:31
  790.2 40.9 %collective-permute-done.15 = f32[1,4096,64]{1,2,0:T(8,128)S(1)} collective-permute-done((f32[1,4096,64]{1,2,0:T(8,128)S(1)}, f32[1,4096,64]{1,2,0:T(8,128)S(1)}, u32[]{:S(2)}, u32[]{:S(2)}) %collective-permute-start.15) | collective-permute-done | bytes 1048608 | tf_op jit(solution)/shard_map/ppermute | solution.py:31
  898.9 55.1 %collective-permute-done.18 = f32[1,4096,64]{1,2,0:T(8,128)S(1)} collective-permute-done((f32[1,4096,64]{1,2,0:T(8,128)S(1)}, f32[1,4096,64]{1,2,0:T(8,128)S(1)}, u32[]{:S(2)}, u32[]{:S(2)}) %collective-permute-start.18) | collective-permute-done | bytes 1048608 | tf_op jit(solution)/shard_map/ppermute | solution.py:31
  954.2 47.6 %collective-permute-start.19 = (f32[1,4096,64]{1,2,0:T(8,128)S(1)}, f32[1,4096,64]{1,2,0:T(8,128)S(1)}, u32[]{:S(2)}, u32[]{:S(2)}) collective-permute-start(f32[1,4096,64]{1,2,0:T(8,128)S(1)} %add.457), channel_id=1, source_target_pairs={{0,8},{1,9},{2,10},{3,11},{4,12},{5,13},{6,14},{7,15},{16,24},{17,... | collective-permute-start | bytes 3145736 | tf_op jit(solution)/shard_map/ppermute | solution.py:31
  1001.8 40.9 %collective-permute-done.19 = f32[1,4096,64]{1,2,0:T(8,128)S(1)} collective-permute-done((f32[1,4096,64]{1,2,0:T(8,128)S(1)}, f32[1,4096,64]{1,2,0:T(8,128)S(1)}, u32[]{:S(2)}, u32[]{:S(2)}) %collective-permute-start.19) | collective-permute-done | bytes 1048608 | tf_op jit(solution)/shard_map/ppermute | solution.py:31
  1110.7 54.7 %collective-permute-done.22 = f32[1,4096,64]{1,2,0:T(8,128)S(1)} collective-permute-done((f32[1,4096,64]{1,2,0:T(8,128)S(1)}, f32[1,4096,64]{1,2,0:T(8,128)S(1)}, u32[]{:S(2)}, u32[]{:S(2)}) %collective-permute-start.22) | collective-permute-done | bytes 1048608 | tf_op jit(solution)/shard_map/ppermute | solution.py:31
  1165.6 47.6 %collective-permute-start.23 = (f32[1,4096,64]{1,2,0:T(8,128)S(1)}, f32[1,4096,64]{1,2,0:T(8,128)S(1)}, u32[]{:S(2)}, u32[]{:S(2)}) collective-permute-start(f32[1,4096,64]{1,2,0:T(8,128)S(1)} %add.469), channel_id=1, source_target_pairs={{0,8},{1,9},{2,10},{3,11},{4,12},{5,13},{6,14},{7,15},{16,24},{17,... | collective-permute-start | bytes 3145736 | tf_op jit(solution)/shard_map/ppermute | solution.py:31
  1213.2 40.9 %collective-permute-done.23 = f32[1,4096,64]{1,2,0:T(8,128)S(1)} collective-permute-done((f32[1,4096,64]{1,2,0:T(8,128)S(1)}, f32[1,4096,64]{1,2,0:T(8,128)S(1)}, u32[]{:S(2)}, u32[]{:S(2)}) %collective-permute-start.23) | collective-permute-done | bytes 1048608 | tf_op jit(solution)/shard_map/ppermute | solution.py:31
  1321.7 55.1 %collective-permute-done.26 = f32[1,4096,64]{1,2,0:T(8,128)S(1)} collective-permute-done((f32[1,4096,64]{1,2,0:T(8,128)S(1)}, f32[1,4096,64]{1,2,0:T(8,128)S(1)}, u32[]{:S(2)}, u32[]{:S(2)}) %collective-permute-start.26) | collective-permute-done | bytes 1048608 | tf_op jit(solution)/shard_map/ppermute | solution.py:31
  1377.0 47.6 %collective-permute-start.27 = (f32[1,4096,64]{1,2,0:T(8,128)S(1)}, f32[1,4096,64]{1,2,0:T(8,128)S(1)}, u32[]{:S(2)}, u32[]{:S(2)}) collective-permute-start(f32[1,4096,64]{1,2,0:T(8,128)S(1)} %add.481), channel_id=1, source_target_pairs={{0,8},{1,9},{2,10},{3,11},{4,12},{5,13},{6,14},{7,15},{16,24},{17,... | collective-permute-start | bytes 3145736 | tf_op jit(solution)/shard_map/ppermute | solution.py:31
  1424.6 40.9 %collective-permute-done.27 = f32[1,4096,64]{1,2,0:T(8,128)S(1)} collective-permute-done((f32[1,4096,64]{1,2,0:T(8,128)S(1)}, f32[1,4096,64]{1,2,0:T(8,128)S(1)}, u32[]{:S(2)}, u32[]{:S(2)}) %collective-permute-start.27) | collective-permute-done | bytes 1048608 | tf_op jit(solution)/shard_map/ppermute | solution.py:31
  1533.2 55.1 %collective-permute-done.30 = f32[1,4096,64]{1,2,0:T(8,128)S(1)} collective-permute-done((f32[1,4096,64]{1,2,0:T(8,128)S(1)}, f32[1,4096,64]{1,2,0:T(8,128)S(1)}, u32[]{:S(2)}, u32[]{:S(2)}) %collective-permute-start.30) | collective-permute-done | bytes 1048608 | tf_op jit(solution)/shard_map/ppermute | solution.py:31
  1588.4 47.8 %collective-permute-start.31 = (f32[1,4096,64]{1,2,0:T(8,128)S(1)}, f32[1,4096,64]{1,2,0:T(8,128)S(1)}, u32[]{:S(2)}, u32[]{:S(2)}) collective-permute-start(f32[1,4096,64]{1,2,0:T(8,128)S(1)} %add.493), channel_id=1, source_target_pairs={{0,8},{1,9},{2,10},{3,11},{4,12},{5,13},{6,14},{7,15},{16,24},{17,... | collective-permute-start | bytes 3145736 | tf_op jit(solution)/shard_map/ppermute | solution.py:31
  1636.2 40.9 %collective-permute-done.31 = f32[1,4096,64]{1,2,0:T(8,128)S(1)} collective-permute-done((f32[1,4096,64]{1,2,0:T(8,128)S(1)}, f32[1,4096,64]{1,2,0:T(8,128)S(1)}, u32[]{:S(2)}, u32[]{:S(2)}) %collective-permute-start.31) | collective-permute-done | bytes 1048608 | tf_op jit(solution)/shard_map/ppermute | solution.py:31
  (106 shorter events, 538.3 us)
Async XLA Ops:
  45.3 25.9 %collective-permute-start.1 = (f32[1,4096,64]{1,2,0:T(8,128)S(1)}, f32[1,4096,64]{1,2,0:T(8,128)S(1)}, u32[]{:S(2)}, u32[]{:S(2)}) collective-permute-start(f32[1,4096,64]{1,2,0:T(8,128)S(1)} %fusion.261), channel_id=1, source_target_pairs={{0,2},{1,3},{2,4},{3,5},{4,6},{5,7},{6,8},{7,9},{8,10},{9,11},{10,... | collective-permute-start | bytes 3145736 | tf_op jit(solution)/shard_map/ppermute | solution.py:31
  71.3 75.4 %collective-permute-start.2 = (f32[1,4096,64]{1,2,0:T(8,128)S(1)}, f32[1,4096,64]{1,2,0:T(8,128)S(1)}, u32[]{:S(2)}, u32[]{:S(2)}) collective-permute-start(f32[1,4096,64]{1,2,0:T(8,128)S(1)} %add.408), channel_id=1, source_target_pairs={{0,4},{1,5},{2,6},{3,7},{4,8},{5,9},{6,10},{7,11},{8,12},{9,13},{1... | collective-permute-start | bytes 3145736 | tf_op jit(solution)/shard_map/ppermute | solution.py:31
  146.8 50.0 %collective-permute-start.3 = (f32[1,4096,64]{1,2,0:T(8,128)S(1)}, f32[1,4096,64]{1,2,0:T(8,128)S(1)}, u32[]{:S(2)}, u32[]{:S(2)}) collective-permute-start(f32[1,4096,64]{1,2,0:T(8,128)S(1)} %add.409), channel_id=1, source_target_pairs={{0,8},{1,9},{2,10},{3,11},{4,12},{5,13},{6,14},{7,15},{16,24},{17,... | collective-permute-start | bytes 3145736 | tf_op jit(solution)/shard_map/ppermute | solution.py:31
  239.2 23.8 %collective-permute-start.5 = (f32[1,4096,64]{1,2,0:T(8,128)S(1)}, f32[1,4096,64]{1,2,0:T(8,128)S(1)}, u32[]{:S(2)}, u32[]{:S(2)}) collective-permute-start(f32[1,4096,64]{1,2,0:T(8,128)S(1)} %fusion.262), channel_id=1, source_target_pairs={{0,2},{1,3},{2,4},{3,5},{4,6},{5,7},{6,8},{7,9},{8,10},{9,11},{10,... | collective-permute-start | bytes 3145736 | tf_op jit(solution)/shard_map/ppermute | solution.py:31
  263.1 56.5 %collective-permute-start.6 = (f32[1,4096,64]{1,2,0:T(8,128)S(1)}, f32[1,4096,64]{1,2,0:T(8,128)S(1)}, u32[]{:S(2)}, u32[]{:S(2)}) collective-permute-start(f32[1,4096,64]{1,2,0:T(8,128)S(1)} %add.420), channel_id=1, source_target_pairs={{0,4},{1,5},{2,6},{3,7},{4,8},{5,9},{6,10},{7,11},{8,12},{9,13},{1... | collective-permute-start | bytes 3145736 | tf_op jit(solution)/shard_map/ppermute | solution.py:31
  319.7 88.5 %collective-permute-start.7 = (f32[1,4096,64]{1,2,0:T(8,128)S(1)}, f32[1,4096,64]{1,2,0:T(8,128)S(1)}, u32[]{:S(2)}, u32[]{:S(2)}) collective-permute-start(f32[1,4096,64]{1,2,0:T(8,128)S(1)} %add.421), channel_id=1, source_target_pairs={{0,8},{1,9},{2,10},{3,11},{4,12},{5,13},{6,14},{7,15},{16,24},{17,... | collective-permute-start | bytes 3145736 | tf_op jit(solution)/shard_map/ppermute | solution.py:31
  450.6 23.8 %collective-permute-start.9 = (f32[1,4096,64]{1,2,0:T(8,128)S(1)}, f32[1,4096,64]{1,2,0:T(8,128)S(1)}, u32[]{:S(2)}, u32[]{:S(2)}) collective-permute-start(f32[1,4096,64]{1,2,0:T(8,128)S(1)} %fusion.263), channel_id=1, source_target_pairs={{0,2},{1,3},{2,4},{3,5},{4,6},{5,7},{6,8},{7,9},{8,10},{9,11},{10,... | collective-permute-start | bytes 3145736 | tf_op jit(solution)/shard_map/ppermute | solution.py:31
  474.5 56.5 %collective-permute-start.10 = (f32[1,4096,64]{1,2,0:T(8,128)S(1)}, f32[1,4096,64]{1,2,0:T(8,128)S(1)}, u32[]{:S(2)}, u32[]{:S(2)}) collective-permute-start(f32[1,4096,64]{1,2,0:T(8,128)S(1)} %add.432), channel_id=1, source_target_pairs={{0,4},{1,5},{2,6},{3,7},{4,8},{5,9},{6,10},{7,11},{8,12},{9,13},{1... | collective-permute-start | bytes 3145736 | tf_op jit(solution)/shard_map/ppermute | solution.py:31
  531.1 88.5 %collective-permute-start.11 = (f32[1,4096,64]{1,2,0:T(8,128)S(1)}, f32[1,4096,64]{1,2,0:T(8,128)S(1)}, u32[]{:S(2)}, u32[]{:S(2)}) collective-permute-start(f32[1,4096,64]{1,2,0:T(8,128)S(1)} %add.433), channel_id=1, source_target_pairs={{0,8},{1,9},{2,10},{3,11},{4,12},{5,13},{6,14},{7,15},{16,24},{17,... | collective-permute-start | bytes 3145736 | tf_op jit(solution)/shard_map/ppermute | solution.py:31
  662.1 23.8 %collective-permute-start.13 = (f32[1,4096,64]{1,2,0:T(8,128)S(1)}, f32[1,4096,64]{1,2,0:T(8,128)S(1)}, u32[]{:S(2)}, u32[]{:S(2)}) collective-permute-start(f32[1,4096,64]{1,2,0:T(8,128)S(1)} %fusion.264), channel_id=1, source_target_pairs={{0,2},{1,3},{2,4},{3,5},{4,6},{5,7},{6,8},{7,9},{8,10},{9,11},{10,... | collective-permute-start | bytes 3145736 | tf_op jit(solution)/shard_map/ppermute | solution.py:31
  685.9 56.5 %collective-permute-start.14 = (f32[1,4096,64]{1,2,0:T(8,128)S(1)}, f32[1,4096,64]{1,2,0:T(8,128)S(1)}, u32[]{:S(2)}, u32[]{:S(2)}) collective-permute-start(f32[1,4096,64]{1,2,0:T(8,128)S(1)} %add.444), channel_id=1, source_target_pairs={{0,4},{1,5},{2,6},{3,7},{4,8},{5,9},{6,10},{7,11},{8,12},{9,13},{1... | collective-permute-start | bytes 3145736 | tf_op jit(solution)/shard_map/ppermute | solution.py:31
  742.6 88.5 %collective-permute-start.15 = (f32[1,4096,64]{1,2,0:T(8,128)S(1)}, f32[1,4096,64]{1,2,0:T(8,128)S(1)}, u32[]{:S(2)}, u32[]{:S(2)}) collective-permute-start(f32[1,4096,64]{1,2,0:T(8,128)S(1)} %add.445), channel_id=1, source_target_pairs={{0,8},{1,9},{2,10},{3,11},{4,12},{5,13},{6,14},{7,15},{16,24},{17,... | collective-permute-start | bytes 3145736 | tf_op jit(solution)/shard_map/ppermute | solution.py:31
  873.7 23.8 %collective-permute-start.17 = (f32[1,4096,64]{1,2,0:T(8,128)S(1)}, f32[1,4096,64]{1,2,0:T(8,128)S(1)}, u32[]{:S(2)}, u32[]{:S(2)}) collective-permute-start(f32[1,4096,64]{1,2,0:T(8,128)S(1)} %fusion.265), channel_id=1, source_target_pairs={{0,2},{1,3},{2,4},{3,5},{4,6},{5,7},{6,8},{7,9},{8,10},{9,11},{10,... | collective-permute-start | bytes 3145736 | tf_op jit(solution)/shard_map/ppermute | solution.py:31
  897.6 56.5 %collective-permute-start.18 = (f32[1,4096,64]{1,2,0:T(8,128)S(1)}, f32[1,4096,64]{1,2,0:T(8,128)S(1)}, u32[]{:S(2)}, u32[]{:S(2)}) collective-permute-start(f32[1,4096,64]{1,2,0:T(8,128)S(1)} %add.456), channel_id=1, source_target_pairs={{0,4},{1,5},{2,6},{3,7},{4,8},{5,9},{6,10},{7,11},{8,12},{9,13},{1... | collective-permute-start | bytes 3145736 | tf_op jit(solution)/shard_map/ppermute | solution.py:31
  954.2 88.4 %collective-permute-start.19 = (f32[1,4096,64]{1,2,0:T(8,128)S(1)}, f32[1,4096,64]{1,2,0:T(8,128)S(1)}, u32[]{:S(2)}, u32[]{:S(2)}) collective-permute-start(f32[1,4096,64]{1,2,0:T(8,128)S(1)} %add.457), channel_id=1, source_target_pairs={{0,8},{1,9},{2,10},{3,11},{4,12},{5,13},{6,14},{7,15},{16,24},{17,... | collective-permute-start | bytes 3145736 | tf_op jit(solution)/shard_map/ppermute | solution.py:31
  1085.1 23.8 %collective-permute-start.21 = (f32[1,4096,64]{1,2,0:T(8,128)S(1)}, f32[1,4096,64]{1,2,0:T(8,128)S(1)}, u32[]{:S(2)}, u32[]{:S(2)}) collective-permute-start(f32[1,4096,64]{1,2,0:T(8,128)S(1)} %fusion.266), channel_id=1, source_target_pairs={{0,2},{1,3},{2,4},{3,5},{4,6},{5,7},{6,8},{7,9},{8,10},{9,11},{10,... | collective-permute-start | bytes 3145736 | tf_op jit(solution)/shard_map/ppermute | solution.py:31
  1108.9 56.5 %collective-permute-start.22 = (f32[1,4096,64]{1,2,0:T(8,128)S(1)}, f32[1,4096,64]{1,2,0:T(8,128)S(1)}, u32[]{:S(2)}, u32[]{:S(2)}) collective-permute-start(f32[1,4096,64]{1,2,0:T(8,128)S(1)} %add.468), channel_id=1, source_target_pairs={{0,4},{1,5},{2,6},{3,7},{4,8},{5,9},{6,10},{7,11},{8,12},{9,13},{1... | collective-permute-start | bytes 3145736 | tf_op jit(solution)/shard_map/ppermute | solution.py:31
  1165.6 88.5 %collective-permute-start.23 = (f32[1,4096,64]{1,2,0:T(8,128)S(1)}, f32[1,4096,64]{1,2,0:T(8,128)S(1)}, u32[]{:S(2)}, u32[]{:S(2)}) collective-permute-start(f32[1,4096,64]{1,2,0:T(8,128)S(1)} %add.469), channel_id=1, source_target_pairs={{0,8},{1,9},{2,10},{3,11},{4,12},{5,13},{6,14},{7,15},{16,24},{17,... | collective-permute-start | bytes 3145736 | tf_op jit(solution)/shard_map/ppermute | solution.py:31
  1296.5 23.8 %collective-permute-start.25 = (f32[1,4096,64]{1,2,0:T(8,128)S(1)}, f32[1,4096,64]{1,2,0:T(8,128)S(1)}, u32[]{:S(2)}, u32[]{:S(2)}) collective-permute-start(f32[1,4096,64]{1,2,0:T(8,128)S(1)} %fusion.267), channel_id=1, source_target_pairs={{0,2},{1,3},{2,4},{3,5},{4,6},{5,7},{6,8},{7,9},{8,10},{9,11},{10,... | collective-permute-start | bytes 3145736 | tf_op jit(solution)/shard_map/ppermute | solution.py:31
  1320.3 56.5 %collective-permute-start.26 = (f32[1,4096,64]{1,2,0:T(8,128)S(1)}, f32[1,4096,64]{1,2,0:T(8,128)S(1)}, u32[]{:S(2)}, u32[]{:S(2)}) collective-permute-start(f32[1,4096,64]{1,2,0:T(8,128)S(1)} %add.480), channel_id=1, source_target_pairs={{0,4},{1,5},{2,6},{3,7},{4,8},{5,9},{6,10},{7,11},{8,12},{9,13},{1... | collective-permute-start | bytes 3145736 | tf_op jit(solution)/shard_map/ppermute | solution.py:31
  1377.0 88.5 %collective-permute-start.27 = (f32[1,4096,64]{1,2,0:T(8,128)S(1)}, f32[1,4096,64]{1,2,0:T(8,128)S(1)}, u32[]{:S(2)}, u32[]{:S(2)}) collective-permute-start(f32[1,4096,64]{1,2,0:T(8,128)S(1)} %add.481), channel_id=1, source_target_pairs={{0,8},{1,9},{2,10},{3,11},{4,12},{5,13},{6,14},{7,15},{16,24},{17,... | collective-permute-start | bytes 3145736 | tf_op jit(solution)/shard_map/ppermute | solution.py:31
  1507.9 23.8 %collective-permute-start.29 = (f32[1,4096,64]{1,2,0:T(8,128)S(1)}, f32[1,4096,64]{1,2,0:T(8,128)S(1)}, u32[]{:S(2)}, u32[]{:S(2)}) collective-permute-start(f32[1,4096,64]{1,2,0:T(8,128)S(1)} %fusion.268), channel_id=1, source_target_pairs={{0,2},{1,3},{2,4},{3,5},{4,6},{5,7},{6,8},{7,9},{8,10},{9,11},{10,... | collective-permute-start | bytes 3145736 | tf_op jit(solution)/shard_map/ppermute | solution.py:31
  1531.8 56.5 %collective-permute-start.30 = (f32[1,4096,64]{1,2,0:T(8,128)S(1)}, f32[1,4096,64]{1,2,0:T(8,128)S(1)}, u32[]{:S(2)}, u32[]{:S(2)}) collective-permute-start(f32[1,4096,64]{1,2,0:T(8,128)S(1)} %add.492), channel_id=1, source_target_pairs={{0,4},{1,5},{2,6},{3,7},{4,8},{5,9},{6,10},{7,11},{8,12},{9,13},{1... | collective-permute-start | bytes 3145736 | tf_op jit(solution)/shard_map/ppermute | solution.py:31
  1588.4 88.6 %collective-permute-start.31 = (f32[1,4096,64]{1,2,0:T(8,128)S(1)}, f32[1,4096,64]{1,2,0:T(8,128)S(1)}, u32[]{:S(2)}, u32[]{:S(2)}) collective-permute-start(f32[1,4096,64]{1,2,0:T(8,128)S(1)} %add.493), channel_id=1, source_target_pairs={{0,8},{1,9},{2,10},{3,11},{4,12},{5,13},{6,14},{7,15},{16,24},{17,... | collective-permute-start | bytes 3145736 | tf_op jit(solution)/shard_map/ppermute | solution.py:31
  (11 other events, 256.2 us)
where the time goes:
time: 1690 us; the launch traced here: 1680 us
  waiting for transfers between devices  1050 us (62%)
  starting transfers between devices  394 us (23%)
  matrix products  202 us (12%)
  other arithmetic  32.7 us (2%)
    ppermute x32, waiting for transfers between devices, body(): lax.ppermute(prefix, 'time', [(source, source + distance) for source in r...  1050 us
    ppermute x32, starting transfers between devices, body(): lax.ppermute(prefix, 'time', [(source, source + distance) for source in r...  394 us
    dot_general x8, matrix products, local_drift(): jnp.einsum('tbnd,dc->tbnc', gelu_out, w_out, preferred_element_type=jnp.f...  202 us
  transfers between devices with their start and end apart: 32, of which 32 were waited for; matrix products, arithmetic and copies ran while one was open for 0% of the time, Pallas kernels for 0%

commit v1 on v0

v1 whole, which is shorter than its diff:
```python
import functools
import math

import jax
import jax.numpy as jnp
from jax import lax
from jax.experimental import pallas as pl
from jax.experimental.pallas import tpu as pltpu
from jax.sharding import PartitionSpec as P

MESH = pl.DeviceIdType.MESH
SWEEPS = 8
HALF = SWEEPS // 2
LANES = 128
BLOCK = 256
GELU_A = 2.0 * math.sqrt(2.0 / math.pi)
GELU_B = 8.0 * math.sqrt(2.0 / math.pi) * 0.044715


def kernel(
    n_time, steps_own, chunks,
    x_hbm, w_in_ref, w_out_ref, mod_ref, step_ref, noise_hbm, out_hbm,
    latents, lat_bf, act, noise_buf, out_buf, x_own, x_full, mod_all, step_all, mod_cols,
    x_sem, full_sem, mod_send, mod_recv, step_send, step_recv, noise_send, noise_recv, out_send, out_recv,
):
    data, me = lax.axis_index("data"), lax.axis_index("time")
    steps = n_time * steps_own
    own = chunks * LANES
    channels = x_own.shape[0]
    hidden = w_in_ref.shape[0]
    half_hidden = hidden // 2
    group = HALF * LANES

    def lane_slice(device, chunk):
        return pl.ds(pl.multiple_of(device * own + chunk * LANES, LANES), LANES)

    def other(i):
        near = i // 2 + 1
        return lax.rem(me + jnp.where(lax.rem(i, 2) == 0, near, n_time - near), n_time)

    def remote(src, dst, send, recv, device):
        return pltpu.make_async_remote_copy(
            src_ref=src, dst_ref=dst, send_sem=send, recv_sem=recv,
            device_id=(data, device), device_id_type=MESH,
        )

    def mod_copy(device, slot):
        return remote(mod_ref, mod_all.at[slot], mod_send.at[device], mod_recv.at[slot], device)

    def step_copy(device, slot):
        return remote(step_ref, step_all.at[slot], step_send.at[device], step_recv.at[slot], device)

    def noise_copy(device, chunk, k, owner):
        return remote(
            noise_hbm.at[k, :, lane_slice(device, chunk)],
            noise_buf.at[chunk, owner * steps_own + k],
            noise_send.at[chunk, k, device],
            noise_recv.at[chunk, owner * steps_own + k],
            device,
        )

    def own_noise(chunk, k):
        return pltpu.make_async_copy(
            noise_hbm.at[k, :, lane_slice(me, chunk)],
            noise_buf.at[chunk, me * steps_own + k],
            noise_recv.at[chunk, me * steps_own + k],
        )

    def out_copy(chunk, j, source):
        return remote(
            out_buf.at[chunk, j],
            out_hbm.at[lax.rem(j, steps_own), :, lane_slice(source, chunk)],
            out_send.at[chunk, j],
            out_recv.at[chunk, lax.rem(j, steps_own), source],
            j // steps_own,
        )

    def own_out(chunk, j):
        return pltpu.make_async_copy(
            out_buf.at[chunk, j],
            out_hbm.at[lax.rem(j, steps_own), :, lane_slice(me, chunk)],
            out_recv.at[chunk, lax.rem(j, steps_own), me],
        )

    x_copy = pltpu.make_async_copy(x_hbm.at[:, pl.ds(pl.multiple_of(me * own, LANES), own)], x_own, x_sem)
    x_copy.start()

    barrier = pltpu.get_barrier_semaphore()

    @pl.loop(0, n_time - 1)
    def _(i):
        pl.semaphore_signal(barrier, inc=1, device_id=(data, other(i)), device_id_type=MESH)

    pl.semaphore_wait(barrier, n_time - 1)

    @pl.loop(0, n_time - 1)
    def _(i):
        mod_copy(other(i), me).start()
        step_copy(other(i), me).start()

    for chunk in range(chunks):
        for k in range(steps_own):
            own_noise(chunk, k).start()

            @pl.loop(0, n_time - 1)
            def _(i, chunk=chunk, k=k):
                noise_copy(other(i), chunk, k, me).start()

    @pl.when(me == 0)
    def _():
        full = pltpu.make_async_copy(x_hbm, x_full, full_sem)
        full.start()
        full.wait()
        pltpu.make_async_copy(x_full, out_hbm.at[0], full_sem).start()

    x_copy.wait()
    mod_all[me] = mod_ref[...]
    step_all[me] = step_ref[...]

    @pl.loop(0, n_time - 1)
    def _(i):
        mod_copy(me, other(i)).wait_recv()
        step_copy(me, other(i)).wait_recv()

    rows = mod_all[...].astype(jnp.float32).reshape(n_time * 8, half_hidden)
    is_scale = lax.rem(lax.broadcasted_iota(jnp.int32, rows.shape, 0), 8) < 2 * steps_own
    mod_cols[...] = (jnp.where(is_scale, 1.0 + rows, rows) * 0.5).T

    def column(block, j, kind):
        per_half = half_hidden // BLOCK
        lane = 8 * (j // steps_own) + 2 * (kind * steps_own + lax.rem(j, steps_own)) + block // per_half
        start = (block % per_half) * BLOCK
        index = jnp.full((BLOCK, LANES), lane, jnp.int32)
        return jnp.take_along_axis(mod_cols[start:start + BLOCK, :], index, axis=1)

    def drift(j, g):
        x_bf = lat_bf[:, g * group:(g + 1) * group]
        for block in range(hidden // BLOCK):
            pre = jnp.dot(w_in_ref[block * BLOCK:(block + 1) * BLOCK, :], x_bf, preferred_element_type=jnp.float32)
            scale = column(block, j, 0)
            shift = column(block, j, 1)
            for t in range(HALF):
                y = pre[:, t * LANES:(t + 1) * LANES] * scale + shift
                u = y * (y * y * GELU_B + GELU_A)
                a = y * jnp.tanh(u) + y
                act[g, block * BLOCK:(block + 1) * BLOCK, t * LANES:(t + 1) * LANES] = a.astype(jnp.bfloat16)
        return jnp.dot(w_out_ref[...], act[g], preferred_element_type=jnp.float32)

    def advance(chunk, j, g, proj, add):
        base = LANES + g * group
        for t in range(HALF):
            part = slice(base + t * LANES, base + (t + 1) * LANES)
            step = step_all[j // steps_own, pl.ds(lax.rem(j, steps_own), 1), :]
            latents[:, part] = latents[:, part] + (step * proj[:, t * LANES:(t + 1) * LANES] + add)

    def emit(chunk, j, slot):
        out_buf[chunk, j] = latents[:, slot * LANES:(slot + 1) * LANES]

    def send(chunk, j):
        @pl.when(j // steps_own == me)
        def _():
            own_out(chunk, j).start()

        @pl.when(j // steps_own != me)
        def _():
            out_copy(chunk, j, me).start()

    def wait_noise(chunk, j):
        @pl.when(j // steps_own == me)
        def _():
            own_noise(chunk, lax.rem(j, steps_own)).wait()

        @pl.when(j // steps_own != me)
        def _():
            noise_copy(me, chunk, lax.rem(j, steps_own), j // steps_own).wait_recv()

    @pl.loop(0, chunks)
    def _(chunk):
        start = x_own[:, pl.ds(pl.multiple_of(chunk * LANES, LANES), LANES)]
        for s in range(SWEEPS + 1):
            latents[:, s * LANES:(s + 1) * LANES] = start

        def one_step(j, groups, slot):
            wait_noise(chunk, j)
            lat_bf[...] = latents[:, :2 * group].astype(jnp.bfloat16)
            add = noise_buf[chunk, j]
            for g in groups:
                advance(chunk, j, g, drift(j, g), add)
            emit(chunk, j + 1, slot)

        @pl.loop(0, HALF)
        def _(j):
            @pl.when(j > 0)
            def _():
                send(chunk, j)

            one_step(j, (0,), HALF)

        reached = latents[:, HALF * LANES:(HALF + 1) * LANES]
        for s in range(HALF + 1, SWEEPS + 1):
            latents[:, s * LANES:(s + 1) * LANES] = reached

        @pl.loop(HALF, steps - 1 - HALF)
        def _(j):
            send(chunk, j)
            one_step(j, (0, 1), SWEEPS)

        @pl.loop(steps - 1 - HALF, steps - 1)
        def _(j):
            send(chunk, j)
            one_step(j, (1,), SWEEPS)

        send(chunk, steps - 1)

    @pl.loop(0, n_time - 1)
    def _(i):
        mod_copy(other(i), me).wait_send()
        step_copy(other(i), me).wait_send()
        for chunk in range(chunks):
            for k in range(steps_own):
                noise_copy(other(i), chunk, k, me).wait_send()

    for chunk in range(chunks):
        wait_noise(chunk, steps - 1)

        @pl.loop(1, steps)
        def _(j, chunk=chunk):
            @pl.when(j // steps_own != me)
            def _():
                out_copy(chunk, j, me).wait_send()

        for k in range(steps_own):
            @pl.loop(0, n_time)
            def _(source, chunk=chunk, k=k):
                j = me * steps_own + k

                @pl.when(j > 0)
                def _():
                    @pl.when(source == me)
                    def _():
                        own_out(chunk, j).wait()

                    @pl.when(source != me)
                    def _():
                        out_copy(chunk, j, source).wait_recv()

    @pl.when(me == 0)
    def _():
        pltpu.make_async_copy(x_full, out_hbm.at[0], full_sem).wait()


def solution(mesh):
    n_time = mesh.shape["time"]

    def body(x_init, w_in, w_out, mod_scale, mod_shift, step_size, noise_inc):
        steps_own, batch, tokens, channels = noise_inc.shape
        hidden = w_in.shape[1]
        own = tokens // n_time
        chunks = own // LANES
        steps = n_time * steps_own
        f32, bf16 = jnp.float32, jnp.bfloat16
        x_t = jnp.transpose(x_init, (0, 2, 1)).reshape(channels, tokens)
        noise_t = jnp.transpose(noise_inc, (0, 1, 3, 2)).reshape(steps_own, channels, tokens)
        mod = jnp.concatenate([mod_scale, mod_shift]).reshape(8, hidden // 2)
        step = jnp.broadcast_to(jnp.pad(step_size, (0, 8 - steps_own))[:, None], (8, LANES))
        vmem = pl.BlockSpec(memory_space=pltpu.VMEM)
        hbm = pl.BlockSpec(memory_space=pl.ANY)
        dma = pltpu.SemaphoreType.DMA
        out = pl.pallas_call(
            functools.partial(kernel, n_time, steps_own, chunks),
            out_shape=jax.ShapeDtypeStruct((steps_own, channels, tokens), f32),
            in_specs=[hbm, vmem, vmem, vmem, vmem, hbm],
            out_specs=hbm,
            scratch_shapes=[
                pltpu.VMEM((channels, (SWEEPS + 1) * LANES), f32),
                pltpu.VMEM((channels, SWEEPS * LANES), bf16),
                pltpu.VMEM((2, hidden, HALF * LANES), bf16),
                pltpu.VMEM((chunks, steps, channels, LANES), f32),
                pltpu.VMEM((chunks, steps, channels, LANES), f32),
                pltpu.VMEM((channels, own), f32),
                pltpu.VMEM((channels, tokens), f32),
                pltpu.VMEM((n_time, 8, hidden // 2), bf16),
                pltpu.VMEM((n_time, 8, LANES), f32),
                pltpu.VMEM((hidden // 2, n_time * 8), f32),
                dma(()), dma(()),
                dma((n_time,)), dma((n_time,)),
                dma((n_time,)), dma((n_time,)),
                dma((chunks, steps_own, n_time)), dma((chunks, steps)),
                dma((chunks, steps)), dma((chunks, steps_own, n_time)),
            ],
            compiler_params=pltpu.CompilerParams(
                collective_id=0, has_side_effects=True, vmem_limit_bytes=48 * 1024 * 1024
            ),
        )(x_t, w_in.T, w_out.T, mod, step, noise_t)
        return jnp.transpose(out.reshape(steps_own, batch, channels, tokens), (0, 1, 3, 2))

    return jax.shard_map(
        body,
        mesh=mesh,
        in_specs=(P("data"), P(), P(), P("time"), P("time"), P("time"), P("time", "data")),
        out_specs=P("time", "data"),
        check_vma=False,
    )
```

time: 1690 us -> 194 us (0.11)
  the two profiles are of different devices: /device:TPU:55 before, /device:TPU:247 now
where the time goes in v1:
time: 194 us
  Pallas kernels  187 us (96%)
  local copies, waits for them, and re-layouts  6.95 us (4%)
    pallas_call x1, Pallas kernels, body(): pl.pallas_call(functools.partial(kernel, n_time, steps_own, chunks), out_...  187 us
    unnamed x8, local copies, waits for them, and re-layouts  6.21 us

profile of v1, /device:TPU:247, one launch (start us, length us, event | category | flops | bytes accessed | tf_op | source)
XLA Modules:
  0.0 194.3 jit_solution(17175292649591405853)
XLA Ops:
  0.0 0.7 pad.4
  0.7 0.1 broadcast_in_dim.2.step_ref
  0.7 0.7 pad_maximum_fusion
  1.5 1.1 copy.8
  2.6 0.0 copy-start
  2.6 1.6 copy-done
  4.2 0.0 copy-start.1
  4.2 1.2 copy-done.1
  5.5 0.0 copy-start.2
  5.5 0.9 copy-done.2
  6.4 186.5 %shard_map.73 = f32[2,64,4096]{2,1,0:T(8,128)S(1)} custom-call(f32[64,4096]{1,0:T(8,128)S(1)} %bitcast.18, bf16[1536,64]{1,0:T(8,128)(2,1)S(1)} %bitcast.17, bf16[64,1536]{1,0:T(8,128)(2,1)S(1)} %bitcast.19, bf16[8,768]{1,0:T(8,128)(2,1)S(1)} %reshape.14.mod_ref, f32[8,128]{1,0:T(8,128)S(1)} %broadcast_in_dim.2.step_ref, f32[2,64,4096]{2,1,0:T(8,128)S(1)} %bitcast.16), custom_call_target="tpu_custom_call" | custom-call | tf_op jit(solution)/shard_map/pallas_call | solution.py:269
  192.9 1.3 copy.12
  (1 shorter events, 0.0 us)
Async XLA Ops:
  2.6 1.6 copy-start
  4.2 1.2 copy-start.1
  5.5 0.9 copy-start.2
